TPU v7x, 32 devices: a whole 2x2x4 slice. The times are simulated.
32 devices in a mesh: row: 4 (over z), vec: 8 (over y, x, core).
Axes of the slice: x: 2, y: 2, z: 4, core: 2. Of those that a mesh axis runs over, the one named last changes fastest.
Arguments:
- vectors: float32 [4096, 4096], P('row', 'vec'), may hold values from -6 to 6
- block_index: int32 [3, 4], replicated, may hold values from 0 to 7
- block_offset: int32 [3, 4], replicated, may hold values from 0 to 3, as said below
- reflector_vectors: float32 [4, 8, 512, 256], P('row', 'vec'), may hold values from -0.25 to 0.25
- reflector_factors: float32 [4, 8, 256, 256], P('row', 'vec'), may hold values from -0.1875 to 0.1875
Outputs:
- updated: float32 [4096, 4096], P('row', 'vec')
Inputs may be any that keep to these rules, and one draw needn't show every extreme that they name: `block_offset`: the last owner's offset is at most 2, so every block lies inside the slab.
All inputs are finite; a program needn't handle non-finite values.
Results may differ from a plain program's by a relative error of at most 0.0001.
Values sent between devices are 32-bit elements; how exact they have to be, the bound alone decides.
No kernel may reach another device: no remote copies, remote signals or barrier semaphores. Data moves between devices by JAX's collectives and lax.ppermute only.
A program may use at most 64 MiB of HBM per device.

v0:
```python
import jax
import jax.numpy as jnp
from jax import lax
from jax.sharding import PartitionSpec as P

FRONTS = 3


def broadcast(value, axis, source):
    kept = jnp.where(lax.axis_index(axis) == source, value, 0).astype(value.dtype)
    return lax.psum(kept, axis)


def passed_along(value, axis, steps):
    count = lax.axis_size(axis)
    first, last = (max(0, -steps), min(count, count - steps))
    return lax.ppermute(value, axis, [(source, source + steps) for source in range(first, last)])


def apply_reflector_block(row_window, vector_matrix, triangular_matrix):
    high_precision = lax.Precision.HIGHEST
    inner_product = jnp.dot(
        vector_matrix.T, row_window, precision=high_precision, preferred_element_type=jnp.float32
    )
    mixed_rows = jnp.dot(
        jnp.triu(triangular_matrix),
        inner_product,
        precision=high_precision,
        preferred_element_type=jnp.float32,
    )
    return row_window - jnp.dot(
        vector_matrix, mixed_rows, precision=high_precision, preferred_element_type=jnp.float32
    )


def body(vectors, block_index, block_offset, reflector_vectors, reflector_factors):
    rows_here = vectors.shape[0]
    width = reflector_vectors.shape[3]
    span = reflector_vectors.shape[2]
    slots = rows_here // width
    owner_index = lax.axis_index("row")
    local_rows = vectors
    for front in range(FRONTS):
        root_owner = block_index[front, owner_index]
        vector_matrix, triangular_matrix = (
            broadcast(reflector_vectors[0, 0], "vec", root_owner),
            broadcast(reflector_factors[0, 0], "vec", root_owner),
        )
        slot = block_offset[front, owner_index]
        crossing = slot == slots - 1
        lower_rows = passed_along(local_rows[:width], "row", -1)
        bottom_row = local_rows[rows_here - width :]
        edge = lax.cond(
            crossing,
            lambda: apply_reflector_block(
                jnp.concatenate([bottom_row, lower_rows], axis=0), vector_matrix, triangular_matrix
            ),
            lambda: jnp.concatenate([bottom_row, lower_rows], axis=0),
        )
        sent = jnp.where(crossing, edge[width:], lower_rows)
        back = passed_along(sent, "row", 1)
        top_rows = jnp.where(owner_index > 0, back, local_rows[:width])
        local_rows = jnp.concatenate([top_rows, local_rows[width:]], axis=0)
        start_row = jnp.minimum(slot, slots - 2) * width

        def own_window():
            row_window = lax.dynamic_slice_in_dim(local_rows, start_row, span, 0)
            return lax.dynamic_update_slice_in_dim(
                local_rows,
                apply_reflector_block(row_window, vector_matrix, triangular_matrix),
                start_row,
                0,
            )

        def crossed_rows():
            return jnp.concatenate([local_rows[: rows_here - width], edge[:width]], axis=0)

        local_rows = lax.cond(crossing, crossed_rows, own_window)
    return local_rows


def solution(mesh):
    return jax.shard_map(
        body,
        mesh=mesh,
        in_specs=(
            P("row", "vec"),
            P(),
            P(),
            P("row", "vec", None, None),
            P("row", "vec", None, None),
        ),
        out_specs=P("row", "vec"),
        check_vma=False,
    )
```

profile of v0, /device:TPU:12, one launch (start us, length us, event | category | flops | bytes accessed | tf_op | source)
XLA Modules:
  0.0 191.9 jit_solution(16495925374914444277)
XLA Ops:
  9.9 2.3 %select_bitcast_fusion = (f32[512,256]{1,0:T(8,128)}, f32[512,256]{1,0:T(8,128)}, f32[512,256]{1,0:T(8,128)}) fusion(f32[1,1,512,256]{3,2,1,0:T(8,128)} %param.20, pred[]{:T(512)S(6)} %eq.26, pred[]{:T(512)S(6)} %eq.24, pred[]{:T(512)S(6)} %eq.25), kind=kLoop, calls=%fused_computation.81 | loop fusion | flops 393216 | bytes 2097155 | tf_op jit(solution)/shard_map/jit(_where)/select_n | solution.py:10
  14.3 2.4 %collective-permute-start = (f32[256,512]{0,1:T(8,128)S(1)}, f32[256,512]{0,1:T(8,128)S(1)}, u32[]{:S(2)}, u32[]{:S(2)}) collective-permute-start(f32[256,512]{0,1:T(8,128)S(1)} %copy.15), channel_id=1, source_target_pairs={{8,0},{16,8},{24,16},{9,1},{17,9},{25,17},{10,2},{18,10},{26,18},{... | collective-permute-start | bytes 1572872 | tf_op jit(solution)/shard_map/ppermute | solution.py:17
  17.5 12.4 %collective-permute-done = f32[256,512]{0,1:T(8,128)S(1)} collective-permute-done((f32[256,512]{0,1:T(8,128)S(1)}, f32[256,512]{0,1:T(8,128)S(1)}, u32[]{:S(2)}, u32[]{:S(2)}) %collective-permute-start) | collective-permute-done | bytes 524320 | tf_op jit(solution)/shard_map/ppermute | solution.py:17
  29.9 47.6 %all-reduce.3.cloned.1.call-done = (f32[256,256]{1,0:T(8,128)}, f32[512,256]{1,0:T(8,128)}, f32[256,256]{1,0:T(8,128)}, f32[512,256]{1,0:T(8,128)}, f32[256,256]{1,0:T(8,128)}, /*index=5*/f32[512,256]{1,0:T(8,128)}) async-done(((f32[256,256]{1,0:T(8,128)}, f32[512,256]{1,0:T(8,128)}, f32[256,256]{1,0:T(8,128)}, f32[512,256]{1,0:T(8,128)}, f32[256,256]{1,0:T(8,128)}, /*index=5*/f32[512,256]{1,0:T(8,128)}), ...) | async-done | bytes 2359312 | tf_op jit(solution)/shard_map/psum | solution.py:11
  77.5 6.6 %conditional.6 = (f32[512,512]{0,1:T(8,128)}, f32[256,512]{0,1:T(8,128)S(1)}) conditional(s32[]{:T(128)} %convert_element_type.22, (f32[256,512]{0,1:T(8,128)S(1)}, f32[256,512]{0,1:T(8,128)S(1)}) %tuple.85, (f32[256,512]{0,1:T(8,128)S(1)}, f32[256,512]{0,1:T(8,128)S(1)}, f32[256,256]{1,0:T(8,128)}, f32[512,256]{1,0:T(8,128)}) %tuple.86), branch_computations={%region_2.3_spmd, %region_3.4_spmd} | conditional | flops 2013659392 | bytes 12847176 | solution.py:53
  80.2 2.9 %fusion = f32[512,512]{0,1:T(8,128)} fusion(f32[512,512]{0,1:T(8,128)S(1)} %constant_dynamic-update-slice_fusion, f32[256,512]{1,0:T(8,128)S(1)} %fusion.1, f32[512,256]{1,0:T(8,128)S(1)} %copy-done.4), kind=kOutput, calls=%fused_computation.2 | convolution fusion | flops 805568512 | bytes 3145728 | tf_op jit(solution)/shard_map/cond/branch_1_fun/dot_general | solution.py:31
  84.2 1.9 %collective-permute-start.1 = (f32[256,512]{0,1:T(8,128)S(1)}, f32[256,512]{0,1:T(8,128)S(1)}, u32[]{:S(2)}, u32[]{:S(2)}) collective-permute-start(f32[256,512]{0,1:T(8,128)S(1)} %broadcast_select_fusion), channel_id=1, source_target_pairs={{0,8},{8,16},{16,24},{1,9},{9,17},{17,25},{2,10},{10,18},{18,26},{... | collective-permute-start | bytes 1572872 | tf_op jit(solution)/shard_map/ppermute | solution.py:17
  89.3 10.2 %collective-permute-done.1 = f32[256,512]{0,1:T(8,128)S(1)} collective-permute-done((f32[256,512]{0,1:T(8,128)S(1)}, f32[256,512]{0,1:T(8,128)S(1)}, u32[]{:S(2)}, u32[]{:S(2)}) %collective-permute-start.1) | collective-permute-done | bytes 524320 | tf_op jit(solution)/shard_map/ppermute | solution.py:17
  100.6 3.5 %conditional.7 = (f32[256,512]{0,1:T(8,128)}, f32[1024,512]{0,1:T(8,128)S(1)}, f32[1024,512]{0,1:T(8,128)S(1)}) conditional(s32[]{:T(128)} %convert_element_type.22, (s32[]{:T(128)}, f32[1024,512]{0,1:T(8,128)S(1)}, f32[256,256]{1,0:T(8,128)}, f32[512,256]{1,0:T(8,128)S(1)}) %tuple.142, (f32[512,512]{0,1:T(8,128)}, f32[1024,512]{0,1:T(8,128)S(1)}) %tuple.88), branch_computations={%region_4.5_spmd, %region_5.6_spmd} | conditional | flops 2013659392 | bytes 12847222 | solution.py:78
  106.2 1.9 collective-permute-start.2
  108.8 12.8 %collective-permute-done.2 = f32[256,512]{0,1:T(8,128)S(1)} collective-permute-done((f32[256,512]{0,1:T(8,128)}, f32[256,512]{0,1:T(8,128)S(1)}, u32[]{:S(2)}, u32[]{:S(2)}) %collective-permute-start.2) | collective-permute-done | bytes 524320 | tf_op jit(solution)/shard_map/ppermute | solution.py:17
  121.6 2.4 %conditional.8 = (f32[512,512]{0,1:T(8,128)}, f32[256,512]{0,1:T(8,128)S(1)}) conditional(s32[]{:T(128)} %convert_element_type.21, (f32[256,512]{0,1:T(8,128)}, f32[256,512]{0,1:T(8,128)S(1)}) %tuple.89, (f32[256,512]{0,1:T(8,128)}, f32[256,512]{0,1:T(8,128)S(1)}, f32[256,256]{1,0:T(8,128)S(1)}, f32[512,256]{1,0:T(8,128)S(1)}) %tuple.145), branch_computations={%region_8.9_spmd, %region_9.10_spmd} | conditional | flops 2013659392 | bytes 9701392 | solution.py:53
  121.6 2.2 %pad_maximum_fusion.2 = f32[512,512]{0,1:T(8,128)} fusion(f32[256,512]{0,1:T(8,128)S(1)} %get-tuple-element.252, f32[256,512]{0,1:T(8,128)} %get-tuple-element.160), kind=kLoop, calls=%fused_computation.26 | loop fusion | flops 262144 | bytes 2097152 | tf_op jit(solution)/shard_map/cond/branch_0_fun/concatenate | solution.py:58
  124.1 3.6 %collective-permute-start.3 = (f32[256,512]{0,1:T(8,128)S(1)}, f32[256,512]{0,1:T(8,128)S(1)}, u32[]{:S(2)}, u32[]{:S(2)}) collective-permute-start(f32[256,512]{0,1:T(8,128)S(1)} %broadcast_select_fusion.1), channel_id=1, source_target_pairs={{0,8},{8,16},{16,24},{1,9},{9,17},{17,25},{2,10},{10,18},{18,26},{... | collective-permute-start | bytes 1572872 | tf_op jit(solution)/shard_map/ppermute | solution.py:17
  127.8 11.7 %collective-permute-done.3 = f32[256,512]{0,1:T(8,128)S(1)} collective-permute-done((f32[256,512]{0,1:T(8,128)S(1)}, f32[256,512]{0,1:T(8,128)S(1)}, u32[]{:S(2)}, u32[]{:S(2)}) %collective-permute-start.3) | collective-permute-done | bytes 524320 | tf_op jit(solution)/shard_map/ppermute | solution.py:17
  141.7 5.3 %conditional.9 = (f32[256,512]{0,1:T(8,128)}, f32[1024,512]{0,1:T(8,128)S(1)}, f32[1024,512]{0,1:T(8,128)S(1)}) conditional(s32[]{:T(128)} %convert_element_type.21, (s32[]{:T(128)}, f32[1024,512]{0,1:T(8,128)S(1)}, f32[256,256]{1,0:T(8,128)}, f32[512,256]{1,0:T(8,128)S(1)}) %tuple.141, (f32[512,512]{0,1:T(8,128)}, ...), branch_computations={%region_10.11_spmd, %region_11.12_spmd} | conditional | flops 2013659392 | bytes 12847222 | solution.py:78
  144.1 1.9 fusion.23
  151.7 10.9 %collective-permute-done.4 = f32[256,512]{0,1:T(8,128)S(1)} collective-permute-done((f32[256,512]{0,1:T(8,128)}, f32[256,512]{0,1:T(8,128)S(1)}, u32[]{:S(2)}, u32[]{:S(2)}) %collective-permute-start.4) | collective-permute-done | bytes 524320 | tf_op jit(solution)/shard_map/ppermute | solution.py:17
  162.7 2.5 %conditional.10 = (f32[512,512]{0,1:T(8,128)}, f32[256,512]{0,1:T(8,128)S(1)}) conditional(s32[]{:T(128)} %convert_element_type.20, (f32[256,512]{0,1:T(8,128)}, f32[256,512]{0,1:T(8,128)S(1)}) %tuple.93, (f32[256,512]{0,1:T(8,128)}, f32[256,512]{0,1:T(8,128)S(1)}, f32[256,256]{1,0:T(8,128)S(1)}, f32[512,256]{1,0:T(8,128)S(1)}) %tuple.143), branch_computations={%region_14.15_spmd, %region_15.16_spmd} | conditional | flops 2013659392 | bytes 9701392 | solution.py:53
  162.7 2.2 %pad_maximum_fusion.4 = f32[512,512]{0,1:T(8,128)} fusion(f32[256,512]{0,1:T(8,128)S(1)} %get-tuple-element.262, f32[256,512]{0,1:T(8,128)} %get-tuple-element.172), kind=kLoop, calls=%fused_computation.52 | loop fusion | flops 262144 | bytes 2097152 | tf_op jit(solution)/shard_map/cond/branch_0_fun/concatenate | solution.py:58
  165.2 1.9 %collective-permute-start.5 = (f32[256,512]{0,1:T(8,128)S(1)}, f32[256,512]{0,1:T(8,128)S(1)}, u32[]{:S(2)}, u32[]{:S(2)}) collective-permute-start(f32[256,512]{0,1:T(8,128)S(1)} %broadcast_select_fusion.2), channel_id=1, source_target_pairs={{0,8},{8,16},{16,24},{1,9},{9,17},{17,25},{2,10},{10,18},{18,26},{... | collective-permute-start | bytes 1572872 | tf_op jit(solution)/shard_map/ppermute | solution.py:17
  167.3 10.4 %collective-permute-done.5 = f32[256,512]{0,1:T(8,128)S(1)} collective-permute-done((f32[256,512]{0,1:T(8,128)S(1)}, f32[256,512]{0,1:T(8,128)S(1)}, u32[]{:S(2)}, u32[]{:S(2)}) %collective-permute-start.5) | collective-permute-done | bytes 524320 | tf_op jit(solution)/shard_map/ppermute | solution.py:17
  179.0 6.0 %conditional.11 = (f32[1024,512]{1,0:T(8,128)}) conditional(s32[]{:T(128)} %convert_element_type.20, (s32[]{:T(128)}, f32[1024,512]{0,1:T(8,128)S(1)}, f32[256,256]{1,0:T(8,128)S(1)}, f32[512,256]{1,0:T(8,128)S(1)}) %tuple.144, (f32[1024,512]{0,1:T(8,128)S(1)}, f32[512,512]{0,1:T(8,128)}) %tuple.96), branch_computations={%region_16.17_spmd, %region_17.18_spmd} | conditional | flops 2013659392 | bytes 12582920 | solution.py:78
  181.3 1.9 fusion.39
  (72 shorter events, 31.5 us)
Async XLA Ops:
  6.5 5.6 %copy-start.14 = (f32[1,1,256,256]{3,2,1,0:T(8,128)S(1)}, f32[1,1,256,256]{3,2,1,0:T(8,128)}, u32[]{:S(2)}) copy-start(f32[1,1,256,256]{3,2,1,0:T(8,128)} %param.21) | copy-start | bytes 786436
  6.5 71.0 %all-reduce.3.cloned.1.call-start = ((), (), s32[]{:S(2)}) async-start(), calls=%async_computation | async-start | bytes 4718592 | tf_op jit(solution)/shard_map/psum | solution.py:11
  12.2 1.9 copy-start.8
  14.3 15.6 %collective-permute-start = (f32[256,512]{0,1:T(8,128)S(1)}, f32[256,512]{0,1:T(8,128)S(1)}, u32[]{:S(2)}, u32[]{:S(2)}) collective-permute-start(f32[256,512]{0,1:T(8,128)S(1)} %copy.15), channel_id=1, source_target_pairs={{8,0},{16,8},{24,16},{9,1},{17,9},{25,17},{10,2},{18,10},{26,18},{... | collective-permute-start | bytes 1572872 | tf_op jit(solution)/shard_map/ppermute | solution.py:17
  77.5 1.0 copy-start.4
  77.5 2.0 %copy-start.12 = (f32[256,256]{1,0:T(8,128)S(1)}, f32[256,256]{1,0:T(8,128)}, u32[]{:S(2)}) copy-start(f32[256,256]{1,0:T(8,128)} %get-tuple-element.152) | copy-start | bytes 786436 | tf_op jit(solution)/shard_map/cond
  84.2 15.3 %collective-permute-start.1 = (f32[256,512]{0,1:T(8,128)S(1)}, f32[256,512]{0,1:T(8,128)S(1)}, u32[]{:S(2)}, u32[]{:S(2)}) collective-permute-start(f32[256,512]{0,1:T(8,128)S(1)} %broadcast_select_fusion), channel_id=1, source_target_pairs={{0,8},{8,16},{16,24},{1,9},{9,17},{17,25},{2,10},{10,18},{18,26},{... | collective-permute-start | bytes 1572872 | tf_op jit(solution)/shard_map/ppermute | solution.py:17
  89.3 10.3 %copy-start.5 = (f32[768,512]{0,1:T(8,128)S(1)}, f32[768,512]{0,1:T(8,128)}, u32[]{:S(2)}) copy-start(f32[768,512]{0,1:T(8,128)} %copy.16) | copy-start | bytes 4718596
  99.6 1.0 copy-start.3
  100.6 20.9 %copy-start.1 = (f32[512,256]{1,0:T(8,128)S(1)}, f32[512,256]{1,0:T(8,128)}, u32[]{:S(2)}) copy-start(f32[512,256]{1,0:T(8,128)} %get-tuple-element.221) | copy-start | bytes 1572868
  100.6 20.9 %copy-start.10 = (f32[256,256]{1,0:T(8,128)S(1)}, f32[256,256]{1,0:T(8,128)}, u32[]{:S(2)}) copy-start(f32[256,256]{1,0:T(8,128)} %get-tuple-element.220) | copy-start | bytes 786436
  104.1 1.3 copy-start.6
  106.2 15.3 %collective-permute-start.2 = (f32[256,512]{0,1:T(8,128)}, f32[256,512]{0,1:T(8,128)S(1)}, u32[]{:S(2)}, u32[]{:S(2)}) collective-permute-start(f32[256,512]{0,1:T(8,128)} %slice.118), channel_id=1, source_target_pairs={{8,0},{16,8},{24,16},{9,1},{17,9},{25,17},{10,2},{18,10},{26,18},{... | collective-permute-start | bytes 1572872 | tf_op jit(solution)/shard_map/ppermute | solution.py:17
  124.1 15.5 %collective-permute-start.3 = (f32[256,512]{0,1:T(8,128)S(1)}, f32[256,512]{0,1:T(8,128)S(1)}, u32[]{:S(2)}, u32[]{:S(2)}) collective-permute-start(f32[256,512]{0,1:T(8,128)S(1)} %broadcast_select_fusion.1), channel_id=1, source_target_pairs={{0,8},{8,16},{16,24},{1,9},{9,17},{17,25},{2,10},{10,18},{18,26},{... | collective-permute-start | bytes 1572872 | tf_op jit(solution)/shard_map/ppermute | solution.py:17
  140.7 1.0 copy-start.2
  141.7 21.0 %copy-start = (f32[512,256]{1,0:T(8,128)S(1)}, f32[512,256]{1,0:T(8,128)}, u32[]{:S(2)}) copy-start(f32[512,256]{1,0:T(8,128)} %get-tuple-element.223) | copy-start | bytes 1572868
  141.7 21.0 %copy-start.9 = (f32[256,256]{1,0:T(8,128)S(1)}, f32[256,256]{1,0:T(8,128)}, u32[]{:S(2)}) copy-start(f32[256,256]{1,0:T(8,128)} %get-tuple-element.222) | copy-start | bytes 786436
  142.4 1.0 copy-start.11
  147.0 1.3 copy-start.7
  149.2 13.5 %collective-permute-start.4 = (f32[256,512]{0,1:T(8,128)}, f32[256,512]{0,1:T(8,128)S(1)}, u32[]{:S(2)}, u32[]{:S(2)}) collective-permute-start(f32[256,512]{0,1:T(8,128)} %slice.119), channel_id=1, source_target_pairs={{8,0},{16,8},{24,16},{9,1},{17,9},{25,17},{10,2},{18,10},{26,18},{... | collective-permute-start | bytes 1572872 | tf_op jit(solution)/shard_map/ppermute | solution.py:17
  165.2 12.4 %collective-permute-start.5 = (f32[256,512]{0,1:T(8,128)S(1)}, f32[256,512]{0,1:T(8,128)S(1)}, u32[]{:S(2)}, u32[]{:S(2)}) collective-permute-start(f32[256,512]{0,1:T(8,128)S(1)} %broadcast_select_fusion.2), channel_id=1, source_target_pairs={{0,8},{8,16},{16,24},{1,9},{9,17},{17,25},{2,10},{10,18},{18,26},{... | collective-permute-start | bytes 1572872 | tf_op jit(solution)/shard_map/ppermute | solution.py:17
Sparse Core Ops, SparseCore 0:
  13.2 64.2 all-reduce.2
where the time goes:
time: 193 us; the launch traced here: 192 us
  waiting for transfers between devices  116 us (60%)
  local copies, waits for them, and re-layouts  19.2 us (10%)
  between operations  17.4 us (9%)
  starting transfers between devices  13.7 us (7%)
  other arithmetic  12.1 us (6%)
  matrix products  11.6 us (6%)
  loops' own time  1.93 us (1%)
    ppermute x6, waiting for transfers between devices, passed_along(): lax.ppermute(value, axis, [(source, source + steps) for source in range(f...  68.4 us
    psum x1, waiting for transfers between devices, broadcast(): return lax.psum(kept, axis)  47.6 us
    ppermute x6, starting transfers between devices, passed_along(): lax.ppermute(value, axis, [(source, source + steps) for source in range(f...  13.7 us
    unnamed x25, local copies, waits for them, and re-layouts  7.18 us
    dot_general x3, matrix products, apply_reflector_block(): jnp.dot(vector_matrix, mixed_rows, precision=high_precision, preferred_el...  6.68 us
    concatenate x2, other arithmetic, body(): jnp.concatenate([bottom_row, lower_rows], axis=0)  4.39 us
  transfers between devices with their start and end apart: 7, of which 7 were waited for; matrix products, arithmetic and copies ran while one was open for 2% of the time, Pallas kernels for 0%

commit v1 on v0

--- a/solution.py
+++ b/solution.py
@@ -8,7 +8,7 @@
 
 def broadcast(value, axis, source):
     kept = jnp.where(lax.axis_index(axis) == source, value, 0).astype(value.dtype)
-    return lax.psum(kept, axis)
+    return jnp.sum(lax.all_gather(kept, axis), axis=0)
 
 
 def passed_along(value, axis, steps):

time: 193 us -> 252 us (1.31)
  waiting for transfers between devices: 116 us -> 161 us
  other arithmetic: 12.1 us -> 26.9 us
  local copies, waits for them, and re-layouts: 19.2 us -> 16.2 us
    all_gather x0 -> x6, waiting for transfers between devices: none -> 107 us  [broadcast(): return jnp.sum(lax.all_gather(kept, axis), axis=0)]
    psum x1 -> x0, waiting for transfers between devices: 47.6 us -> none  [broadcast(): return lax.psum(kept, axis)]
    ppermute x6, waiting for transfers between devices: 68.4 us -> 52.5 us  [passed_along(): lax.ppermute(value, axis, [(source, source + steps) for source in range(f...]
    reduce_sum x0 -> x6, other arithmetic: none -> 12.8 us  [broadcast(): return jnp.sum(lax.all_gather(kept, axis), axis=0)]
    unnamed x25 -> x11, local copies, waits for them, and re-layouts: 7.18 us -> 5.69 us
  transfers between devices with their start and end apart: 7 -> 12, of which waited for: 7 -> 8; matrix products, arithmetic and copies ran while one was open for 2% -> 16% of each run, Pallas kernels for 0% -> 0%
where the time goes in v1:
time: 252 us; the launch traced here: 250 us
  waiting for transfers between devices  161 us (64%)
  other arithmetic  26.9 us (11%)
  between operations  17.4 us (7%)
  local copies, waits for them, and re-layouts  16.2 us (6%)
  starting transfers between devices  15.1 us (6%)
  matrix products  11.6 us (5%)
    all_gather x6, waiting for transfers between devices, broadcast(): return jnp.sum(lax.all_gather(kept, axis), axis=0)  107 us
    ppermute x6, waiting for transfers between devices, passed_along(): lax.ppermute(value, axis, [(source, source + steps) for source in range(f...  52.5 us
    ppermute x6, starting transfers between devices, passed_along(): lax.ppermute(value, axis, [(source, source + steps) for source in range(f...  14.9 us
    reduce_sum x6, other arithmetic, broadcast(): return jnp.sum(lax.all_gather(kept, axis), axis=0)  12.8 us
    dot_general x3, matrix products, apply_reflector_block(): jnp.dot(vector_matrix, mixed_rows, precision=high_precision, preferred_el...  6.71 us
    unnamed x11, local copies, waits for them, and re-layouts  5.69 us
  transfers between devices with their start and end apart: 12, of which 8 were waited for; matrix products, arithmetic and copies ran while one was open for 16% of the time, Pallas kernels for 0%

profile of v1, /device:TPU:12, one launch (start us, length us, event | category | flops | bytes accessed | tf_op | source)
XLA Modules:
  0.0 250.3 jit_solution(202398072631426686)
XLA Ops:
  11.8 2.4 broadcast_select_fusion
  18.8 2.4 collective-permute-start
  22.1 12.3 %collective-permute-done = f32[256,512]{0,1:T(8,128)S(1)} collective-permute-done((f32[256,512]{0,1:T(8,128)S(1)}, f32[256,512]{0,1:T(8,128)S(1)}, u32[]{:S(2)}, u32[]{:S(2)}) %collective-permute-start) | collective-permute-done | bytes 524320 | tf_op jit(solution)/shard_map/ppermute | solution.py:17
  34.4 6.3 %all-gather.13.cloned.1.call-done = f32[8,1,256,256]{3,2,1,0:T(8,128)} async-done(((f32[1,1,256,256]{3,2,1,0:T(8,128)}), f32[8,1,256,256]{3,2,1,0:T(8,128)}) %all-gather.13.cloned.1.call-update) | async-done | bytes 2097168 | tf_op jit(solution)/shard_map/all_gather | solution.py:11
  42.5 36.7 %all-gather.15.cloned.1.call-done = f32[8,1,512,256]{3,2,1,0:T(8,128)} async-done(((f32[1,1,512,256]{3,2,1,0:T(8,128)}), f32[8,1,512,256]{3,2,1,0:T(8,128)}) %all-gather.15.cloned.1.call-update) | async-done | bytes 4194320 | tf_op jit(solution)/shard_map/all_gather | solution.py:11
  79.1 2.5 %reduce_sum.55 = f32[512,256]{1,0:T(8,128)S(1)} reduce(f32[8,1,512,256]{3,2,1,0:T(8,128)} %all-gather.15.cloned.1.call-done, f32[]{:T(128)} %constant.73.clone.1), dimensions={0,1}, to_apply=%region_0.1 | reduce | flops 917504 | bytes 4718596 | tf_op jit(solution)/shard_map/reduce_sum | solution.py:11
  81.6 5.8 %conditional.6 = (f32[512,512]{0,1:T(8,128)}, f32[256,512]{0,1:T(8,128)S(1)}) conditional(s32[]{:T(128)} %convert_element_type.22, (f32[256,512]{0,1:T(8,128)S(1)}, f32[256,512]{0,1:T(8,128)S(1)}) %tuple.85, (f32[256,512]{0,1:T(8,128)S(1)}, f32[256,512]{0,1:T(8,128)S(1)}, f32[256,256]{1,0:T(8,128)S(1)}, f32[512,256]{1,0:T(8,128)S(1)}) %tuple.86), branch_computations={%region_2.3_spmd, %region_3.4_spmd} | conditional | flops 2013659392 | bytes 9701392 | solution.py:53
  83.5 2.9 %fusion = f32[512,512]{0,1:T(8,128)} fusion(f32[512,512]{0,1:T(8,128)S(1)} %constant_dynamic-update-slice_fusion, f32[256,512]{1,0:T(8,128)S(1)} %fusion.1, f32[512,256]{1,0:T(8,128)S(1)} %get-tuple-element.153), kind=kOutput, calls=%fused_computation.2 | convolution fusion | flops 805568512 | bytes 3145728 | tf_op jit(solution)/shard_map/cond/branch_1_fun/dot_general | solution.py:31
  91.9 12.6 %collective-permute-done.1 = f32[256,512]{0,1:T(8,128)S(1)} collective-permute-done((f32[256,512]{0,1:T(8,128)}, f32[256,512]{0,1:T(8,128)S(1)}, u32[]{:S(2)}, u32[]{:S(2)}) %collective-permute-start.1) | collective-permute-done | bytes 524320 | tf_op jit(solution)/shard_map/ppermute | solution.py:17
  104.8 3.5 %conditional.7 = (f32[256,512]{0,1:T(8,128)}, f32[1024,512]{0,1:T(8,128)S(1)}, f32[1024,512]{0,1:T(8,128)S(1)}) conditional(s32[]{:T(128)} %convert_element_type.22, (s32[]{:T(128)}, f32[1024,512]{0,1:T(8,128)S(1)}, f32[256,256]{1,0:T(8,128)S(1)}, f32[512,256]{1,0:T(8,128)S(1)}) %tuple.87, (f32[512,512]{0,1:T(8,128)}, f32[1024,512]{0,1:T(8,128)S(1)}) %tuple.88), branch_computations={%region_4.5_spmd, %region_5.6_spmd} | conditional | flops 2013659392 | bytes 12582936 | solution.py:78
  114.7 32.5 %all-gather.19.cloned.1.call-done = f32[8,1,512,256]{3,2,1,0:T(8,128)} async-done(((f32[1,1,512,256]{3,2,1,0:T(8,128)}), f32[8,1,512,256]{3,2,1,0:T(8,128)}) %all-gather.19.cloned.1.call-update) | async-done | bytes 4194320 | tf_op jit(solution)/shard_map/all_gather | solution.py:11
  147.2 2.5 %reduce_sum.57 = f32[512,256]{1,0:T(8,128)S(1)} reduce(f32[8,1,512,256]{3,2,1,0:T(8,128)} %all-gather.19.cloned.1.call-done, f32[]{:T(128)} %constant.73.clone.1), dimensions={0,1}, to_apply=%region_6.7 | reduce | flops 917504 | bytes 4718596 | tf_op jit(solution)/shard_map/reduce_sum | solution.py:11
  149.7 2.5 conditional.8
  149.7 2.2 pad_maximum_fusion.2
  152.3 3.4 %collective-permute-start.3 = (f32[256,512]{0,1:T(8,128)S(1)}, f32[256,512]{0,1:T(8,128)S(1)}, u32[]{:S(2)}, u32[]{:S(2)}) collective-permute-start(f32[256,512]{0,1:T(8,128)S(1)} %broadcast_select_fusion.4), channel_id=1, source_target_pairs={{0,8},{8,16},{16,24},{1,9},{9,17},{17,25},{2,10},{10,18},{18,26},{... | collective-permute-start | bytes 1572872 | tf_op jit(solution)/shard_map/ppermute | solution.py:17
  155.8 15.2 %collective-permute-done.3 = f32[256,512]{0,1:T(8,128)S(1)} collective-permute-done((f32[256,512]{0,1:T(8,128)S(1)}, f32[256,512]{0,1:T(8,128)S(1)}, u32[]{:S(2)}, u32[]{:S(2)}) %collective-permute-start.3) | collective-permute-done | bytes 524320 | tf_op jit(solution)/shard_map/ppermute | solution.py:17
  172.3 5.1 %conditional.9 = (f32[256,512]{0,1:T(8,128)}, f32[1024,512]{0,1:T(8,128)S(1)}, f32[1024,512]{0,1:T(8,128)S(1)}) conditional(s32[]{:T(128)} %convert_element_type.21, (s32[]{:T(128)}, f32[1024,512]{0,1:T(8,128)S(1)}, f32[256,256]{1,0:T(8,128)S(1)}, f32[512,256]{1,0:T(8,128)S(1)}) %tuple.91, (f32[512,512]{0,1:T(8,128)}, ...), branch_computations={%region_10.11_spmd, %region_11.12_spmd} | conditional | flops 2013659392 | bytes 12582936 | solution.py:78
  183.9 31.2 %all-gather.23.cloned.1.call-done = f32[8,1,512,256]{3,2,1,0:T(8,128)} async-done(((f32[1,1,512,256]{3,2,1,0:T(8,128)}), f32[8,1,512,256]{3,2,1,0:T(8,128)}) %all-gather.23.cloned.1.call-update) | async-done | bytes 4194320 | tf_op jit(solution)/shard_map/all_gather | solution.py:11
  215.1 2.5 %reduce_sum.59 = f32[512,256]{1,0:T(8,128)S(1)} reduce(f32[8,1,512,256]{3,2,1,0:T(8,128)} %all-gather.23.cloned.1.call-done, f32[]{:T(128)} %constant.73.clone.1), dimensions={0,1}, to_apply=%region_12.13 | reduce | flops 917504 | bytes 4718596 | tf_op jit(solution)/shard_map/reduce_sum | solution.py:11
  217.6 2.5 conditional.10
  217.6 2.2 pad_maximum_fusion.4
  220.1 3.4 %collective-permute-start.5 = (f32[256,512]{0,1:T(8,128)S(1)}, f32[256,512]{0,1:T(8,128)S(1)}, u32[]{:S(2)}, u32[]{:S(2)}) collective-permute-start(f32[256,512]{0,1:T(8,128)S(1)} %broadcast_select_fusion.5), channel_id=1, source_target_pairs={{0,8},{8,16},{16,24},{1,9},{9,17},{17,25},{2,10},{10,18},{18,26},{... | collective-permute-start | bytes 1572872 | tf_op jit(solution)/shard_map/ppermute | solution.py:17
  223.7 12.4 %collective-permute-done.5 = f32[256,512]{0,1:T(8,128)S(1)} collective-permute-done((f32[256,512]{0,1:T(8,128)S(1)}, f32[256,512]{0,1:T(8,128)S(1)}, u32[]{:S(2)}, u32[]{:S(2)}) %collective-permute-start.5) | collective-permute-done | bytes 524320 | tf_op jit(solution)/shard_map/ppermute | solution.py:17
  237.5 6.0 %conditional.11 = (f32[1024,512]{1,0:T(8,128)}) conditional(s32[]{:T(128)} %convert_element_type.20, (s32[]{:T(128)}, f32[1024,512]{0,1:T(8,128)S(1)}, f32[256,256]{1,0:T(8,128)S(1)}, f32[512,256]{1,0:T(8,128)S(1)}) %tuple.95, (f32[1024,512]{0,1:T(8,128)S(1)}, f32[512,512]{0,1:T(8,128)}) %tuple.96), branch_computations={%region_16.17_spmd, %region_17.18_spmd} | conditional | flops 2013659392 | bytes 12582920 | solution.py:78
  (74 shorter events, 45.6 us)
Async XLA Ops:
  6.5 34.2 %all-gather.13.cloned.1.call-start = ((), (), s32[]{:S(2)}) async-start(), calls=%async_computation | async-start | bytes 2359296 | tf_op jit(solution)/shard_map/all_gather | solution.py:11
  11.7 5.0 %copy-start = (f32[1024,512]{1,0:T(8,128)S(1)}, f32[1024,512]{1,0:T(8,128)}, u32[]{:S(2)}) copy-start(f32[1024,512]{1,0:T(8,128)} %param.17) | copy-start | bytes 6291460
  11.7 67.4 %all-gather.15.cloned.1.call-start = ((), (), s32[]{:S(2)}) async-start(), calls=%async_computation.1 | async-start | bytes 4718592 | tf_op jit(solution)/shard_map/all_gather | solution.py:11
  14.2 98.7 %all-gather.17.cloned.1.call-start = ((), (), s32[]{:S(2)}) async-start(), calls=%async_computation.2 | async-start | bytes 2359296 | tf_op jit(solution)/shard_map/all_gather | solution.py:11
  14.9 132.2 %all-gather.19.cloned.1.call-start = ((), (), s32[]{:S(2)}) async-start(), calls=%async_computation.3 | async-start | bytes 4718592 | tf_op jit(solution)/shard_map/all_gather | solution.py:11
  15.5 166.6 %all-gather.21.cloned.1.call-start = ((), (), s32[]{:S(2)}) async-start(), calls=%async_computation.4 | async-start | bytes 2359296 | tf_op jit(solution)/shard_map/all_gather | solution.py:11
  16.1 199.0 %all-gather.23.cloned.1.call-start = ((), (), s32[]{:S(2)}) async-start(), calls=%async_computation.5 | async-start | bytes 4718592 | tf_op jit(solution)/shard_map/all_gather | solution.py:11
  18.8 15.6 %collective-permute-start = (f32[256,512]{0,1:T(8,128)S(1)}, f32[256,512]{0,1:T(8,128)S(1)}, u32[]{:S(2)}, u32[]{:S(2)}) collective-permute-start(f32[256,512]{0,1:T(8,128)S(1)} %copy.19), channel_id=1, source_target_pairs={{8,0},{16,8},{24,16},{9,1},{17,9},{25,17},{10,2},{18,10},{26,18},{... | collective-permute-start | bytes 1572872 | tf_op jit(solution)/shard_map/ppermute | solution.py:17
  87.4 2.8 %slice-start = ((f32[1024,512]{1,0:T(8,128)}), f32[768,512]{1,0:T(8,128)S(1)}, s32[]{:S(2)}) async-start(f32[1024,512]{1,0:T(8,128)} %param.17), calls=%async_computation.6 | async-start | bytes 3145728 | tf_op jit(solution)/shard_map/slice | solution.py:63
  88.3 16.1 %collective-permute-start.1 = (f32[256,512]{0,1:T(8,128)}, f32[256,512]{0,1:T(8,128)S(1)}, u32[]{:S(2)}, u32[]{:S(2)}) collective-permute-start(f32[256,512]{0,1:T(8,128)} %broadcast_select_fusion.3), channel_id=1, source_target_pairs={{0,8},{8,16},{16,24},{1,9},{9,17},{17,25},{2,10},{10,18},{18,26},{... | collective-permute-start | bytes 1572872 | tf_op jit(solution)/shard_map/ppermute | solution.py:17
  91.9 12.7 %copy-start.1 = (f32[768,512]{0,1:T(8,128)S(1)}, f32[768,512]{0,1:T(8,128)}, u32[]{:S(2)}) copy-start(f32[768,512]{0,1:T(8,128)} %copy.20) | copy-start | bytes 4718596
  108.3 1.3 copy-start.2
  110.4 39.3 %collective-permute-start.2 = (f32[256,512]{0,1:T(8,128)}, f32[256,512]{0,1:T(8,128)S(1)}, u32[]{:S(2)}, u32[]{:S(2)}) collective-permute-start(f32[256,512]{0,1:T(8,128)} %slice.118), channel_id=1, source_target_pairs={{8,0},{16,8},{24,16},{9,1},{17,9},{25,17},{10,2},{18,10},{26,18},{... | collective-permute-start | bytes 1572872 | tf_op jit(solution)/shard_map/ppermute | solution.py:17
  152.3 18.7 %collective-permute-start.3 = (f32[256,512]{0,1:T(8,128)S(1)}, f32[256,512]{0,1:T(8,128)S(1)}, u32[]{:S(2)}, u32[]{:S(2)}) collective-permute-start(f32[256,512]{0,1:T(8,128)S(1)} %broadcast_select_fusion.4), channel_id=1, source_target_pairs={{0,8},{8,16},{16,24},{1,9},{9,17},{17,25},{2,10},{10,18},{18,26},{... | collective-permute-start | bytes 1572872 | tf_op jit(solution)/shard_map/ppermute | solution.py:17
  177.5 1.3 copy-start.3
  179.6 38.0 %collective-permute-start.4 = (f32[256,512]{0,1:T(8,128)}, f32[256,512]{0,1:T(8,128)S(1)}, u32[]{:S(2)}, u32[]{:S(2)}) collective-permute-start(f32[256,512]{0,1:T(8,128)} %slice.119), channel_id=1, source_target_pairs={{8,0},{16,8},{24,16},{9,1},{17,9},{25,17},{10,2},{18,10},{26,18},{... | collective-permute-start | bytes 1572872 | tf_op jit(solution)/shard_map/ppermute | solution.py:17
  220.1 16.0 %collective-permute-start.5 = (f32[256,512]{0,1:T(8,128)S(1)}, f32[256,512]{0,1:T(8,128)S(1)}, u32[]{:S(2)}, u32[]{:S(2)}) collective-permute-start(f32[256,512]{0,1:T(8,128)S(1)} %broadcast_select_fusion.5), channel_id=1, source_target_pairs={{0,8},{8,16},{16,24},{1,9},{9,17},{17,25},{2,10},{10,18},{18,26},{... | collective-permute-start | bytes 1572872 | tf_op jit(solution)/shard_map/ppermute | solution.py:17
Sparse Core Ops, SparseCore 0:
  11.8 28.8 all-gather.12
  42.6 36.4 all-gather.14
  81.0 27.8 all-gather.16
  110.6 36.4 all-gather.18
  148.9 27.8 all-gather.20
  178.5 36.4 all-gather.22
